TPU v7x, 32 devices: a whole 2x2x4 slice. The times are simulated.
32 devices in a mesh: cp: 16 (over z, y, core), vocab: 2 (over x).
Axes of the slice: x: 2, y: 2, z: 4, core: 2. Of those that a mesh axis runs over, the one named last changes fastest.
Arguments:
- queries: bfloat16 [2048, 4096], P('cp', 'vocab'), may hold values from -160 to 160
- key_states: bfloat16 [2048, 1024], P('cp', 'vocab'), may hold values from -6 to 6
- value_states: bfloat16 [2048, 1024], P('cp', 'vocab'), may hold values from -6 to 6
- out_grad: bfloat16 [2048, 4096], P('cp', 'vocab'), may hold values from -6 to 6
- o_weight: bfloat16 [4096, 4096], P('vocab'), may hold values from -0.09375 to 0.09375
- span_order: int32 [32], replicated, may hold values from 0 to 31, each once
Outputs:
- query_grad: float32 [2048, 4096], P('cp', 'vocab')
- key_grad: float32 [2048, 1024], P('cp', 'vocab')
- value_grad: float32 [2048, 1024], P('cp', 'vocab')
Inputs may be any that keep to these rules, and one draw needn't show every extreme that they name: `span_order`: each of the 32 span indices once.
All inputs are finite; a program needn't handle non-finite values.
Results may differ from a plain program's by a relative error of at most 0.014.
Values may be sent and summed in bfloat16 or wider, within the bound.
A program may use at most 64 MiB of HBM per device.

v0:
```python
import functools

import jax
import jax.numpy as jnp
from jax import lax
from jax.experimental import pallas as pl
from jax.experimental.pallas import tpu as pltpu
from jax.sharding import PartitionSpec as P

HEADS = 32
KV_HEADS = 8
HEAD_DIM = 128


def positions(span_order, span_rows):
    offsets = jnp.arange(span_rows, dtype=jnp.int32)
    return (span_order[:, None] * span_rows + offsets[None, :]).reshape(-1)


def block_scores(query_block, key_block, query_places, key_places, factor):
    scores = (
        jnp.einsum("qkgd,skd->kgqs", query_block, key_block, preferred_element_type=jnp.float32)
        * factor
    )
    visible = key_places[None, :] <= query_places[:, None]
    return jnp.where(visible, scores, -jnp.inf)


def local(queries, key_states, value_states, out_grad, o_weight, span_order):
    own_rows = queries.shape[0]
    kv_width = key_states.shape[1]
    kv_heads = kv_width // HEAD_DIM
    groups = HEADS // KV_HEADS
    factor = HEAD_DIM ** (-0.5)
    upstream = lax.dot_general(
        lax.all_gather(out_grad, "vocab", axis=1, tiled=True),
        o_weight,
        (((1,), (1,)), ((), ())),
        preferred_element_type=jnp.float32,
    ).astype(jnp.bfloat16)
    places = positions(span_order, own_rows // 2)
    seq_len = places.shape[0]
    own_places = lax.dynamic_slice_in_dim(places, lax.axis_index("cp") * own_rows, own_rows, 0)
    query_heads = queries.reshape(own_rows, kv_heads, groups, HEAD_DIM)
    upstream_heads = upstream.reshape(own_rows, kv_heads, groups, HEAD_DIM)
    key_all, value_all = (
        lax.all_gather(key_states, "cp", axis=0, tiled=True),
        lax.all_gather(value_states, "cp", axis=0, tiled=True),
    )
    key_all = key_all.reshape(seq_len, kv_heads, HEAD_DIM)
    value_all = value_all.reshape(seq_len, kv_heads, HEAD_DIM)
    block_rows = own_rows * 8
    block_count = seq_len // block_rows
    block_ids = jnp.arange(block_count, dtype=jnp.int32)
    stat_shape = (kv_heads, groups, own_rows)

    def key_block(block_index):
        offset = block_index * block_rows
        return (
            lax.dynamic_slice_in_dim(key_all, offset, block_rows, 0),
            lax.dynamic_slice_in_dim(value_all, offset, block_rows, 0),
            lax.dynamic_slice_in_dim(places, offset, block_rows, 0),
        )

    def stats_step(carried, block_index):
        running, totals, delta_acc = carried
        keys_now, values_now, places_now = key_block(block_index)
        scores = block_scores(query_heads, keys_now, own_places, places_now, factor)
        newest = jnp.maximum(running, jnp.max(scores, axis=3))
        rescale = jnp.exp(running - newest)
        raised = jnp.exp(scores - newest[..., None])
        grad_probs = jnp.einsum(
            "qkgd,skd->kgqs", upstream_heads, values_now, preferred_element_type=jnp.float32
        )
        totals = totals * rescale + jnp.sum(raised, axis=3)
        delta_acc = delta_acc * rescale + jnp.sum(raised * grad_probs, axis=3)
        return ((newest, totals, delta_acc), None)

    start_stats = (
        jnp.full(stat_shape, -1e30, jnp.float32),
        jnp.zeros(stat_shape, jnp.float32),
        jnp.zeros(stat_shape, jnp.float32),
    )
    (running, totals, delta_acc), unused = lax.scan(stats_step, start_stats, block_ids)
    logsum = running + jnp.log(totals)
    deltas = delta_acc / totals

    def grad_pieces(block_index):
        keys_now, values_now, places_now = key_block(block_index)
        scores = block_scores(query_heads, keys_now, own_places, places_now, factor)
        weights = jnp.exp(scores - logsum[..., None])
        grad_probs = jnp.einsum(
            "qkgd,skd->kgqs", upstream_heads, values_now, preferred_element_type=jnp.float32
        )
        grad_scores = (weights * (grad_probs - deltas[..., None])).astype(jnp.bfloat16)
        return (keys_now, weights, grad_scores)

    query_zeros = jnp.zeros((own_rows, kv_heads, groups, HEAD_DIM), jnp.float32)

    def grad_step(carried, block_index):
        keys_now, weights, grad_scores = grad_pieces(block_index)
        carried = (
            carried
            + jnp.einsum(
                "kgqs,skd->qkgd", grad_scores, keys_now, preferred_element_type=jnp.float32
            )
            * factor
        )
        key_term = (
            jnp.einsum(
                "kgqs,qkgd->skd", grad_scores, query_heads, preferred_element_type=jnp.float32
            )
            * factor
        )
        value_term = jnp.einsum(
            "kgqs,qkgd->skd",
            weights.astype(jnp.bfloat16),
            upstream_heads,
            preferred_element_type=jnp.float32,
        )
        joined = jnp.concatenate(
            (key_term.reshape(block_rows, kv_width), value_term.reshape(block_rows, kv_width)),
            axis=1,
        )
        return (carried, joined)

    query_total, stacked = lax.scan(grad_step, query_zeros, block_ids)
    terms = stacked.reshape(seq_len, 2 * kv_width)
    mine = lax.psum_scatter(
        terms.astype(jnp.bfloat16), "cp", scatter_dimension=0, tiled=True
    ).astype(jnp.float32)
    key_grad = mine[:, :kv_width]
    value_grad = mine[:, kv_width:]
    query_grad = query_total.reshape(own_rows, kv_heads * groups * HEAD_DIM)
    return (query_grad, key_grad, value_grad)


MESH = pl.DeviceIdType.MESH
NT = (((1,), (1,)), ((), ()))
NN = (((1,), (0,)), ((), ()))
TILE = 256


def dot(a, b, dims):
    return lax.dot_general(a, b, dims, preferred_element_type=jnp.float32)


def greet(peers):
    barrier = pltpu.get_barrier_semaphore()
    for peer in peers:
        pl.semaphore_signal(barrier, inc=1, device_id=peer, device_id_type=MESH)
    pl.semaphore_wait(barrier, len(peers))


def send_kernel(
    n, kv_heads, q_ref, k_ref, v_ref, g_ref, w_ref, q_all, k_all, v_all, u_all,
    own_g, other_g, own_w, other_w, partial, u_buf,
    send_sem, recv_sem, q_sems, u_sems, own_sem, w_sem, g_sem, gx_sem,
):
    me = lax.axis_index("cp")
    half = lax.axis_index("vocab")
    mine = lax.rem(me, kv_heads)
    plane = me - mine
    width = g_ref.shape[1]
    wide = width // kv_heads
    cut = wide // 2
    offsets = list(range(kv_heads // 2, kv_heads)) + list(range(kv_heads // 2 - 1, -1, -1))
    steps = [(o, part) for o in offsets for part in range(2)]

    def member(o):
        return lax.rem(mine + o, kv_heads)

    def w_copy(t, own):
        o, part = steps[t]
        side = half if own else 1 - half
        return pltpu.make_async_copy(
            w_ref.at[
                pl.ds(pl.multiple_of(member(o) * wide + part * cut, cut), cut),
                pl.ds(pl.multiple_of(side * width, width), width),
            ],
            (own_w if own else other_w).at[t],
            w_sem.at[0 if own else 1, t],
        )

    own_g_copy = pltpu.make_async_copy(g_ref, own_g, g_sem)
    own_g_copy.start()
    for t in range(len(steps)):
        w_copy(t, True).start()
    for t in range(len(steps)):
        w_copy(t, False).start()

    greet([{"cp": lax.rem(me + s, n)} for s in range(1, n)] + [{"vocab": 1 - half}])

    g_copy = pltpu.make_async_remote_copy(
        src_ref=g_ref, dst_ref=other_g, send_sem=gx_sem.at[0], recv_sem=gx_sem.at[1],
        device_id={"vocab": 1 - half}, device_id_type=MESH,
    )
    g_copy.start()

    def columns(ref, at, size):
        return ref.at[:, pl.ds(pl.multiple_of(at * size, size), size)]

    def q_copy(o):
        to = member(o)
        return pltpu.make_async_remote_copy(
            src_ref=columns(q_ref, to, wide), dst_ref=q_all.at[mine],
            send_sem=q_sems.at[0, o], recv_sem=q_sems.at[1, o],
            device_id={"cp": plane + to}, device_id_type=MESH,
        )

    def u_copy(t):
        o, part = steps[t]
        return pltpu.make_async_remote_copy(
            src_ref=u_buf.at[t], dst_ref=u_all.at[mine, :, pl.ds(part * cut, cut)],
            send_sem=u_sems.at[0, t], recv_sem=u_sems.at[1, t],
            device_id={"cp": plane + member(o)}, device_id_type=MESH,
        )

    def kv_copies(s):
        peer = lax.rem(me + s, n)
        head = lax.rem(peer, kv_heads)
        return [
            pltpu.make_async_remote_copy(
                src_ref=columns(source, head, HEAD_DIM), dst_ref=target.at[me],
                send_sem=send_sem.at[i, s], recv_sem=recv_sem.at[i, s],
                device_id={"cp": peer}, device_id_type=MESH,
            )
            for i, (source, target) in enumerate(((k_ref, k_all), (v_ref, v_all)))
        ]

    def start_kv(s, carry):
        for copy in kv_copies(s):
            copy.start()
        return carry

    for o in offsets[:-1]:
        q_copy(o).start()
    lax.fori_loop(1, n, start_kv, 0)
    own_copies = [
        pltpu.make_async_copy(columns(q_ref, mine, wide), q_all.at[mine], own_sem.at[0]),
        pltpu.make_async_copy(columns(k_ref, mine, HEAD_DIM), k_all.at[me], own_sem.at[1]),
        pltpu.make_async_copy(columns(v_ref, mine, HEAD_DIM), v_all.at[me], own_sem.at[2]),
    ]
    for copy in own_copies:
        copy.start()

    own_g_copy.wait()
    for t in range(len(steps)):
        w_copy(t, True).wait()
        partial[t] = dot(own_g[...], own_w[t], NT)
    g_copy.wait()
    for t, (o, part) in enumerate(steps):
        w_copy(t, False).wait()
        block = (partial[t] + dot(other_g[...], other_w[t], NT)).astype(jnp.bfloat16)
        if o == 0:
            u_all[mine, :, pl.ds(part * cut, cut)] = block
        else:
            u_buf[t] = block
            u_copy(t).start()

    def wait_kv(s, carry):
        for copy in kv_copies(s):
            copy.wait()
        return carry

    lax.fori_loop(1, n, wait_kv, 0)
    for o in offsets[:-1]:
        q_copy(o).wait()
    for t, (o, part) in enumerate(steps):
        if o != 0:
            u_copy(t).wait()
    for copy in own_copies:
        copy.wait()


def attend_kernel(
    order_ref, q_ref, k_ref, v_ref, u_ref, dq_out, dkv_out,
    places, ks, vs, k_turned, s_buf, p_buf, dk_sum, dv_sum,
):
    plane = lax.axis_index("cp") // q_ref.shape[0]
    own_rows = q_ref.shape[1]
    groups = q_ref.shape[2] // HEAD_DIM
    seq = k_ref.shape[0]
    spans = order_ref.shape[0]
    rows = seq // spans
    tile = groups * rows
    own_spans = q_ref.shape[0] * own_rows // rows
    per_block = own_rows // rows
    factor = HEAD_DIM ** (-0.5)
    scale = factor * 1.4426950408889634

    for r in range(spans):
        places[order_ref[r]] = r
    for j in range(spans):
        source = pl.ds(pl.multiple_of(places[j] * rows, rows), rows)
        for target, ref in ((ks, k_ref), (vs, v_ref)):
            target[pl.ds(j * rows, rows), :] = ref[source, :]
    k_turned[...] = ks[...].T
    dk_sum[...] = jnp.zeros_like(dk_sum)
    dv_sum[...] = jnp.zeros_like(dv_sum)

    def fold(x, op):
        return op(x.reshape(TILE // 8, 8, tile), axis=0)

    key_at = lax.broadcasted_iota(jnp.int32, (TILE, tile), 0)
    query_at = lax.rem(lax.broadcasted_iota(jnp.int32, (TILE, tile), 1), rows)

    def one_span(t, carry):
        block = t // per_block
        own = pl.ds(pl.multiple_of(lax.rem(t, per_block) * rows, rows), rows)
        start = order_ref[plane * own_spans + t] * rows

        def stacked(ref):
            return jnp.concatenate(
                [ref[block, own, h * HEAD_DIM : (h + 1) * HEAD_DIM] for h in range(groups)], axis=0
            )

        def with_keys(last):
            q_tile = stacked(q_ref)
            u_tile = stacked(u_ref)
            peak = None
            for j in range(last + 1):
                keys = pl.ds(j * TILE, TILE)
                s = dot(ks[keys, :], q_tile, NT)
                if j == last:
                    s = jnp.where(key_at + (last * TILE - start) <= query_at, s, -1e30)
                s_buf[keys, :] = s
                top = fold(s, jnp.max)
                peak = top if peak is None else jnp.maximum(peak, top)
            peak = jnp.max(peak, axis=0, keepdims=True)
            total = jnp.zeros((8, tile), jnp.float32)
            delta = jnp.zeros((8, tile), jnp.float32)
            for j in range(last + 1):
                keys = pl.ds(j * TILE, TILE)
                p = jnp.exp2((s_buf[keys, :] - peak) * scale)
                dp = dot(vs[keys, :], u_tile, NT)
                total = total + fold(p, jnp.sum)
                delta = delta + fold(p * dp, jnp.sum)
                s_buf[keys, :] = p
                p_buf[keys, :] = dp
            inverse = 1.0 / jnp.sum(total, axis=0, keepdims=True)
            delta = jnp.sum(delta, axis=0, keepdims=True) * inverse
            turned = None
            for j in range(last + 1):
                keys = pl.ds(j * TILE, TILE)
                w = s_buf[keys, :] * inverse
                g = (w * (p_buf[keys, :] - delta)).astype(jnp.bfloat16)
                dk_sum[keys, :] += dot(g, q_tile, NN)
                dv_sum[keys, :] += dot(w.astype(jnp.bfloat16), u_tile, NN)
                part = dot(k_turned[:, keys], g, NN)
                turned = part if turned is None else turned + part
            dq = (turned.T * factor).astype(jnp.bfloat16)
            for h in range(groups):
                dq_out[block, own, h * HEAD_DIM : (h + 1) * HEAD_DIM] = dq[h * rows : (h + 1) * rows]

        for last in range(seq // TILE):
            pl.when(start // TILE == last)(functools.partial(with_keys, last))
        return carry

    lax.fori_loop(0, own_spans, one_span, 0)
    for r in range(spans):
        source = pl.ds(pl.multiple_of(order_ref[r] * rows, rows), rows)
        target = pl.ds(r * rows, rows)
        dkv_out[target, :HEAD_DIM] = (dk_sum[source, :] * factor).astype(jnp.bfloat16)
        dkv_out[target, HEAD_DIM:] = dv_sum[source, :].astype(jnp.bfloat16)


def return_kernel(
    kv_heads, dq_ref, dkv_ref, dq_all, dkv_all,
    relay, summed, send_sem, recv_sem, relay_sems, q_sems, own_sem,
):
    me = lax.axis_index("cp")
    mine = lax.rem(me, kv_heads)
    plane = me // kv_heads
    pair = plane + 1 - 2 * lax.rem(plane, 2)
    across = lax.rem(plane + 2, 4)
    pair_across = lax.rem(pair + 2, 4)
    wide = dq_ref.shape[2]
    n = 4 * kv_heads
    greet([{"cp": lax.rem(me + s, n)} for s in range(1, n)])
    own_columns = pl.ds(pl.multiple_of(mine * wide, wide), wide)

    def relay_copy(m):
        return pltpu.make_async_remote_copy(
            src_ref=dkv_ref.at[pair_across * kv_heads + m], dst_ref=relay.at[m],
            send_sem=relay_sems.at[0, m], recv_sem=relay_sems.at[1, m],
            device_id={"cp": pair * kv_heads + mine}, device_id_type=MESH,
        )

    def dkv_copy(kind, m, source):
        to = (plane, pair, across)[kind] * kv_heads + m
        return pltpu.make_async_remote_copy(
            src_ref=dkv_ref.at[to] if source is None else source,
            dst_ref=dkv_all.at[kind * kv_heads + mine],
            send_sem=send_sem.at[kind, m], recv_sem=recv_sem.at[kind, mine],
            device_id={"cp": to}, device_id_type=MESH,
        )

    def arrived(kind, g):
        slot = dkv_all.at[kind * kv_heads + g]
        pltpu.make_async_remote_copy(
            src_ref=slot, dst_ref=slot,
            send_sem=send_sem.at[kind, g], recv_sem=recv_sem.at[kind, g],
            device_id={"cp": pair * kv_heads + mine}, device_id_type=MESH,
        ).wait_recv()

    def dq_copy(o):
        to = lax.rem(mine + o, kv_heads)
        return pltpu.make_async_remote_copy(
            src_ref=dq_ref.at[to], dst_ref=dq_all.at[:, own_columns],
            send_sem=q_sems.at[0, o], recv_sem=q_sems.at[1, o],
            device_id={"cp": plane * kv_heads + to}, device_id_type=MESH,
        )

    others = [lax.rem(mine + o, kv_heads) for o in range(1, kv_heads)]
    for m in range(kv_heads):
        relay_copy(m).start()
    for o in range(1, kv_heads):
        dq_copy(o).start()
    own = pltpu.make_async_copy(dq_ref.at[mine], dq_all.at[:, own_columns], own_sem)
    own.start()
    for m in range(kv_heads):
        relay_copy(m).wait_recv()
        total = dkv_ref[across * kv_heads + m].astype(jnp.float32) + relay[m].astype(jnp.float32)
        summed[m] = total.astype(jnp.bfloat16)
        dkv_copy(2, m, summed.at[m]).start()
        dkv_copy(1, m, None).start()
    for m in others:
        dkv_copy(0, m, None).start()
    dkv_all[mine] = dkv_ref[me]

    for m in range(kv_heads):
        relay_copy(m).wait_send()
        dkv_copy(2, m, summed.at[m]).wait_send()
        dkv_copy(1, m, None).wait_send()
        arrived(1, m)
        arrived(2, m)
    for m in others:
        dkv_copy(0, m, None).wait_send()
        arrived(0, m)
    for o in range(1, kv_heads):
        dq_copy(o).wait()
    own.wait()


def by_planes(n, queries, key_states, value_states, out_grad, o_weight, span_order):
    own_rows, width = queries.shape
    kv_heads = key_states.shape[1] // HEAD_DIM
    wide = width // kv_heads
    cut = wide // 2
    seq = own_rows * n
    tile = (HEADS // KV_HEADS) * (seq // span_order.shape[0])
    hbm_spec = pl.BlockSpec(memory_space=pltpu.HBM)
    vmem_spec = pl.BlockSpec(memory_space=pltpu.VMEM)
    smem_spec = pl.BlockSpec(memory_space=pltpu.SMEM)
    dma = pltpu.SemaphoreType.DMA
    low = jnp.bfloat16
    q_block = jax.ShapeDtypeStruct((kv_heads, own_rows, wide), low)
    kv_block = jax.ShapeDtypeStruct((n, own_rows, HEAD_DIM), low)
    q_all, k_all, v_all, u_all = pl.pallas_call(
        functools.partial(send_kernel, n, kv_heads),
        out_shape=(q_block, kv_block, kv_block, q_block),
        in_specs=[hbm_spec] * 5,
        out_specs=(vmem_spec,) * 4,
        scratch_shapes=[
            pltpu.VMEM((own_rows, width), low),
            pltpu.VMEM((own_rows, width), low),
            pltpu.VMEM((2 * kv_heads, cut, width), low),
            pltpu.VMEM((2 * kv_heads, cut, width), low),
            pltpu.VMEM((2 * kv_heads, own_rows, cut), jnp.float32),
            pltpu.VMEM((2 * kv_heads, own_rows, cut), low),
            dma((2, n)),
            dma((2, n)),
            dma((2, kv_heads)),
            dma((2, 2 * kv_heads)),
            dma((3,)),
            dma((2, 2 * kv_heads)),
            dma(()),
            dma((2,)),
        ],
        compiler_params=pltpu.CompilerParams(
            collective_id=0, has_side_effects=True, vmem_limit_bytes=40 << 20
        ),
        name="send_heads",
    )(queries, key_states, value_states, out_grad, o_weight)
    dq, dkv = pl.pallas_call(
        attend_kernel,
        out_shape=(q_block, jax.ShapeDtypeStruct((seq, 2 * HEAD_DIM), low)),
        in_specs=[smem_spec] + [vmem_spec] * 4,
        out_specs=(vmem_spec,) * 2,
        scratch_shapes=[pltpu.SMEM(span_order.shape, jnp.int32)]
        + [pltpu.VMEM((seq, HEAD_DIM), low)] * 2
        + [pltpu.VMEM((HEAD_DIM, seq), low)]
        + [pltpu.VMEM((seq, tile), jnp.float32)] * 2
        + [pltpu.VMEM((seq, HEAD_DIM), jnp.float32)] * 2,
        compiler_params=pltpu.CompilerParams(vmem_limit_bytes=40 << 20),
        name="attend",
    )(span_order, q_all, k_all.reshape(seq, HEAD_DIM), v_all.reshape(seq, HEAD_DIM), u_all)
    term = (own_rows, 2 * HEAD_DIM)
    dq_all, dkv_all = pl.pallas_call(
        functools.partial(return_kernel, kv_heads),
        out_shape=(
            jax.ShapeDtypeStruct((own_rows, width), low),
            jax.ShapeDtypeStruct((3 * kv_heads,) + term, low),
        ),
        in_specs=[pl.BlockSpec(memory_space=pl.ANY), vmem_spec],
        out_specs=(vmem_spec,) * 2,
        scratch_shapes=[pltpu.VMEM((kv_heads,) + term, low)] * 2
        + [
            dma((3, kv_heads)),
            dma((3, kv_heads)),
            dma((2, kv_heads)),
            dma((2, kv_heads)),
            dma(()),
        ],
        compiler_params=pltpu.CompilerParams(
            collective_id=1, has_side_effects=True, vmem_limit_bytes=16 << 20
        ),
        name="return_grads",
    )(dq, dkv.reshape((n,) + term))

    def over_planes(part):
        heads = [
            sum(part[d].astype(jnp.float32) for d in range(g, 3 * kv_heads, kv_heads)) for g in range(kv_heads)
        ]
        return jnp.concatenate(heads, axis=1)

    return (
        dq_all.astype(jnp.float32),
        over_planes(dkv_all[:, :, :HEAD_DIM]),
        over_planes(dkv_all[:, :, HEAD_DIM:]),
    )


def solution(mesh):
    n = mesh.shape["cp"]
    planes = mesh.shape["vocab"] == 2 and n == 4 * (KV_HEADS // 2)
    body = functools.partial(by_planes, n) if planes else local
    return jax.shard_map(
        body,
        mesh=mesh,
        in_specs=(
            P("cp", "vocab"),
            P("cp", "vocab"),
            P("cp", "vocab"),
            P("cp", "vocab"),
            P("vocab", None),
            P(),
        ),
        out_specs=(P("cp", "vocab"), P("cp", "vocab"), P("cp", "vocab")),
        check_vma=False,
    )
```

profile of v0, /device:TPU:13, one launch (start us, length us, event | category | flops | bytes accessed | tf_op | source)
XLA Modules:
  0.0 71.1 jit_solution(15639688251941472884)
XLA Ops:
  0.6 0.0 copy-start
  0.6 1.0 %copy-done = bf16[128,2048]{1,0:T(8,128)(2,1)S(1)} copy-done((bf16[128,2048]{1,0:T(8,128)(2,1)S(1)}, bf16[128,2048]{1,0:T(8,128)(2,1)}, u32[]{:S(2)}) %copy-start) | copy-done | bytes 524312
  1.7 0.0 copy-start.1
  1.7 1.0 %copy-done.1 = bf16[128,2048]{1,0:T(8,128)(2,1)S(1)} copy-done((bf16[128,2048]{1,0:T(8,128)(2,1)S(1)}, bf16[128,2048]{1,0:T(8,128)(2,1)}, u32[]{:S(2)}) %copy-start.1) | copy-done | bytes 524312
  2.7 0.0 copy-start.2
  2.7 0.9 %copy-done.2 = bf16[128,512]{1,0:T(8,128)(2,1)S(1)} copy-done((bf16[128,512]{1,0:T(8,128)(2,1)S(1)}, bf16[128,512]{1,0:T(8,128)(2,1)}, u32[]{:S(2)}) %copy-start.2) | copy-done | bytes 131096
  3.6 0.0 copy-start.3
  3.6 0.9 %copy-done.3 = bf16[128,512]{1,0:T(8,128)(2,1)S(1)} copy-done((bf16[128,512]{1,0:T(8,128)(2,1)S(1)}, bf16[128,512]{1,0:T(8,128)(2,1)}, u32[]{:S(2)}) %copy-start.3) | copy-done | bytes 131096
  4.5 0.0 copy-start.4
  4.5 28.7 %send_heads.1 = (bf16[4,128,512]{2,1,0:T(8,128)(2,1)S(1)}, bf16[16,128,128]{2,1,0:T(8,128)(2,1)S(1)}, bf16[16,128,128]{2,1,0:T(8,128)(2,1)S(1)}, bf16[4,128,512]{2,1,0:T(8,128)(2,1)S(1)}) custom-call(bf16[128,2048]{1,0:T(8,128)(2,1)S(1)} %copy-done, bf16[128,512]{1,0:T(8,128)(2,1)S(1)} %copy-done.2, bf16[128,512]{1,0:T(8,128)(2,1)S(1)} %copy-done.3, ...), custom_call_target="tpu_custom_call" | custom-call | tf_op jit(solution)/shard_map/send_heads/pallas_call | solution.py:460
  33.3 0.0 copy-done.4
  33.3 11.2 %attend.1 = (bf16[4,128,512]{2,1,0:T(8,128)(2,1)S(1)}, bf16[2048,256]{1,0:T(8,128)(2,1)S(1)}) custom-call(s32[32]{0:T(128)S(1)} %copy-done.4, bf16[4,128,512]{2,1,0:T(8,128)(2,1)S(1)} %get-tuple-element.11.q_ref, bf16[2048,128]{1,0:T(8,128)(2,1)S(1)} %bitcast.20, bf16[2048,128]{1,0:T(8,128)(2,1)S(1)} %bitcast.21, ...), custom_call_target="tpu_custom_call" | custom-call | tf_op jit(solution)/shard_map/attend/pallas_call | solution.py:486
  44.5 24.6 %return_grads.1 = (bf16[128,2048]{1,0:T(8,128)(2,1)S(1)}, bf16[12,128,256]{2,1,0:T(8,128)(2,1)S(1)}) custom-call(bf16[4,128,512]{2,1,0:T(8,128)(2,1)S(1)} %get-tuple-element.15.dq_ref, bf16[16,128,256]{2,1,0:T(8,128)(2,1)S(1)} %bitcast.19), custom_call_target="tpu_custom_call" | custom-call | tf_op jit(solution)/shard_map/return_grads/pallas_call | solution.py:500
  69.1 0.1 add_bitcast_fusion.3
  69.2 0.8 %pad_maximum_fusion = (f32[128,512]{1,0:T(8,128)}, f32[128,512]{1,0:T(8,128)}) fusion(f32[128,128]{1,0:T(8,128)S(1)} %get-tuple-element.23, f32[128,128]{1,0:T(8,128)S(1)} %get-tuple-element.26, f32[128,128]{1,0:T(8,128)S(1)} %get-tuple-element.22, f32[128,128]{1,0:T(8,128)S(1)} %get-tuple-element.25, f32[128,128]{1,0:T(8,128)S(1)} %get-tuple-element.21, ...), kind=kLoop, calls=%fused_computation | loop fusion | flops 393216 | bytes 1048576 | tf_op jit(solution)/shard_map/concatenate | solution.py:526
  70.0 1.1 %convert_element_type.99 = f32[128,2048]{1,0:T(8,128)} convert(bf16[128,2048]{1,0:T(8,128)(2,1)S(1)} %get-tuple-element.17) | non-fusion elementwise | flops 262144 | bytes 1572864 | tf_op jit(solution)/shard_map/convert_element_type | solution.py:529
  (1 shorter events, 0.0 us)
Async XLA Ops:
  0.6 1.0 %copy-start = (bf16[128,2048]{1,0:T(8,128)(2,1)S(1)}, bf16[128,2048]{1,0:T(8,128)(2,1)}, u32[]{:S(2)}) copy-start(bf16[128,2048]{1,0:T(8,128)(2,1)} %q_ref.1) | copy-start | bytes 1572868
  1.7 1.0 %copy-start.1 = (bf16[128,2048]{1,0:T(8,128)(2,1)S(1)}, bf16[128,2048]{1,0:T(8,128)(2,1)}, u32[]{:S(2)}) copy-start(bf16[128,2048]{1,0:T(8,128)(2,1)} %g_ref.1) | copy-start | bytes 1572868
  2.7 0.9 %copy-start.2 = (bf16[128,512]{1,0:T(8,128)(2,1)S(1)}, bf16[128,512]{1,0:T(8,128)(2,1)}, u32[]{:S(2)}) copy-start(bf16[128,512]{1,0:T(8,128)(2,1)} %k_ref.1) | copy-start | bytes 393220
  3.6 0.9 %copy-start.3 = (bf16[128,512]{1,0:T(8,128)(2,1)S(1)}, bf16[128,512]{1,0:T(8,128)(2,1)}, u32[]{:S(2)}) copy-start(bf16[128,512]{1,0:T(8,128)(2,1)} %v_ref.1) | copy-start | bytes 393220
  4.5 28.7 %copy-start.4 = (s32[32]{0:T(128)S(1)}, s32[32]{0:T(128)}, u32[]{:S(2)}) copy-start(s32[32]{0:T(128)} %order_ref.1) | copy-start | bytes 388
where the time goes:
time: 72.6 us; the launch traced here: 71.1 us
  Pallas kernels  64.5 us (89%)
  local copies, waits for them, and re-layouts  3.89 us (5%)
  other arithmetic  2 us (3%)
    pallas_call x1, Pallas kernels, by_planes(): pl.pallas_call(functools.partial(send_kernel, n, kv_heads), out_shape=(q_...  28.7 us
    pallas_call x1, Pallas kernels, by_planes(): pl.pallas_call(functools.partial(return_kernel, kv_heads), out_shape=(jax...  24.6 us
    pallas_call x1, Pallas kernels, by_planes(): pl.pallas_call(attend_kernel, out_shape=(q_block, jax.ShapeDtypeStruct((s...  11.2 us
    unnamed x10, local copies, waits for them, and re-layouts  3.89 us

commit v1 on v0

v1 whole, which is shorter than its diff:
```python
import functools

import jax
import jax.numpy as jnp
from jax import lax
from jax.experimental import pallas as pl
from jax.experimental.pallas import tpu as pltpu
from jax.sharding import PartitionSpec as P

HEADS = 32
KV_HEADS = 8
HEAD_DIM = 128


def positions(span_order, span_rows):
    offsets = jnp.arange(span_rows, dtype=jnp.int32)
    return (span_order[:, None] * span_rows + offsets[None, :]).reshape(-1)


def block_scores(query_block, key_block, query_places, key_places, factor):
    scores = (
        jnp.einsum("qkgd,skd->kgqs", query_block, key_block, preferred_element_type=jnp.float32)
        * factor
    )
    visible = key_places[None, :] <= query_places[:, None]
    return jnp.where(visible, scores, -jnp.inf)


def local(queries, key_states, value_states, out_grad, o_weight, span_order):
    own_rows = queries.shape[0]
    kv_width = key_states.shape[1]
    kv_heads = kv_width // HEAD_DIM
    groups = HEADS // KV_HEADS
    factor = HEAD_DIM ** (-0.5)
    upstream = lax.dot_general(
        lax.all_gather(out_grad, "vocab", axis=1, tiled=True),
        o_weight,
        (((1,), (1,)), ((), ())),
        preferred_element_type=jnp.float32,
    ).astype(jnp.bfloat16)
    places = positions(span_order, own_rows // 2)
    seq_len = places.shape[0]
    own_places = lax.dynamic_slice_in_dim(places, lax.axis_index("cp") * own_rows, own_rows, 0)
    query_heads = queries.reshape(own_rows, kv_heads, groups, HEAD_DIM)
    upstream_heads = upstream.reshape(own_rows, kv_heads, groups, HEAD_DIM)
    key_all, value_all = (
        lax.all_gather(key_states, "cp", axis=0, tiled=True),
        lax.all_gather(value_states, "cp", axis=0, tiled=True),
    )
    key_all = key_all.reshape(seq_len, kv_heads, HEAD_DIM)
    value_all = value_all.reshape(seq_len, kv_heads, HEAD_DIM)
    block_rows = own_rows * 8
    block_count = seq_len // block_rows
    block_ids = jnp.arange(block_count, dtype=jnp.int32)
    stat_shape = (kv_heads, groups, own_rows)

    def key_block(block_index):
        offset = block_index * block_rows
        return (
            lax.dynamic_slice_in_dim(key_all, offset, block_rows, 0),
            lax.dynamic_slice_in_dim(value_all, offset, block_rows, 0),
            lax.dynamic_slice_in_dim(places, offset, block_rows, 0),
        )

    def stats_step(carried, block_index):
        running, totals, delta_acc = carried
        keys_now, values_now, places_now = key_block(block_index)
        scores = block_scores(query_heads, keys_now, own_places, places_now, factor)
        newest = jnp.maximum(running, jnp.max(scores, axis=3))
        rescale = jnp.exp(running - newest)
        raised = jnp.exp(scores - newest[..., None])
        grad_probs = jnp.einsum(
            "qkgd,skd->kgqs", upstream_heads, values_now, preferred_element_type=jnp.float32
        )
        totals = totals * rescale + jnp.sum(raised, axis=3)
        delta_acc = delta_acc * rescale + jnp.sum(raised * grad_probs, axis=3)
        return ((newest, totals, delta_acc), None)

    start_stats = (
        jnp.full(stat_shape, -1e30, jnp.float32),
        jnp.zeros(stat_shape, jnp.float32),
        jnp.zeros(stat_shape, jnp.float32),
    )
    (running, totals, delta_acc), unused = lax.scan(stats_step, start_stats, block_ids)
    logsum = running + jnp.log(totals)
    deltas = delta_acc / totals

    def grad_pieces(block_index):
        keys_now, values_now, places_now = key_block(block_index)
        scores = block_scores(query_heads, keys_now, own_places, places_now, factor)
        weights = jnp.exp(scores - logsum[..., None])
        grad_probs = jnp.einsum(
            "qkgd,skd->kgqs", upstream_heads, values_now, preferred_element_type=jnp.float32
        )
        grad_scores = (weights * (grad_probs - deltas[..., None])).astype(jnp.bfloat16)
        return (keys_now, weights, grad_scores)

    query_zeros = jnp.zeros((own_rows, kv_heads, groups, HEAD_DIM), jnp.float32)

    def grad_step(carried, block_index):
        keys_now, weights, grad_scores = grad_pieces(block_index)
        carried = (
            carried
            + jnp.einsum(
                "kgqs,skd->qkgd", grad_scores, keys_now, preferred_element_type=jnp.float32
            )
            * factor
        )
        key_term = (
            jnp.einsum(
                "kgqs,qkgd->skd", grad_scores, query_heads, preferred_element_type=jnp.float32
            )
            * factor
        )
        value_term = jnp.einsum(
            "kgqs,qkgd->skd",
            weights.astype(jnp.bfloat16),
            upstream_heads,
            preferred_element_type=jnp.float32,
        )
        joined = jnp.concatenate(
            (key_term.reshape(block_rows, kv_width), value_term.reshape(block_rows, kv_width)),
            axis=1,
        )
        return (carried, joined)

    query_total, stacked = lax.scan(grad_step, query_zeros, block_ids)
    terms = stacked.reshape(seq_len, 2 * kv_width)
    mine = lax.psum_scatter(
        terms.astype(jnp.bfloat16), "cp", scatter_dimension=0, tiled=True
    ).astype(jnp.float32)
    key_grad = mine[:, :kv_width]
    value_grad = mine[:, kv_width:]
    query_grad = query_total.reshape(own_rows, kv_heads * groups * HEAD_DIM)
    return (query_grad, key_grad, value_grad)


MESH = pl.DeviceIdType.MESH
NT = (((1,), (1,)), ((), ()))
NN = (((1,), (0,)), ((), ()))
TILE = 256


def dot(a, b, dims):
    return lax.dot_general(a, b, dims, preferred_element_type=jnp.float32)


def neighbours(mine):
    partner = mine + 1 - 2 * lax.rem(mine, 2)
    return [mine, partner, lax.rem(mine + 2, 4), lax.rem(partner + 2, 4)]


def signal(peer):
    pl.semaphore_signal(
        pltpu.get_barrier_semaphore(), inc=1, device_id=peer, device_id_type=MESH
    )


def columns(ref, at, size):
    return ref.at[:, pl.ds(pl.multiple_of(at * size, size), size)]


def send_kernel(
    planes, kv_heads, cuts, q_ref, k_ref, v_ref, g_ref, w_ref, q_all, k_all, v_all, u_all,
    own_q, own_k, own_v, own_g, other_g, own_w, other_w, partial, u_buf,
    load_sem, own_sem, w_sem, g_sem, plane_sem, line_sem, kv_sem, q_sems, u_sems,
):
    me = lax.axis_index("cp")
    half = lax.axis_index("vocab")
    mine = lax.rem(me, kv_heads)
    plane = me // kv_heads
    first = plane * kv_heads
    end = planes - 1
    width = g_ref.shape[1]
    wide = width // kv_heads
    cut = wide // 2
    peers = neighbours(mine)
    order = [2, 3, 1, 0]
    steps = [(idx, part) for idx in order for part in range(2)]

    def w_copy(t, own):
        idx, part = steps[t]
        side = half if own else 1 - half
        return pltpu.make_async_copy(
            w_ref.at[
                pl.ds(pl.multiple_of(peers[idx] * wide + part * cut, cut), cut),
                pl.ds(pl.multiple_of(side * width, width), width),
            ],
            (own_w if own else other_w).at[t],
            w_sem.at[0 if own else 1, t],
        )

    loads = [
        pltpu.make_async_copy(source, target, load_sem.at[i])
        for i, (source, target) in enumerate(
            ((g_ref, own_g), (k_ref, own_k), (v_ref, own_v), (q_ref, own_q))
        )
    ]
    for copy in loads:
        copy.start()
    own_copies = [
        pltpu.make_async_copy(columns(q_ref, mine, wide), q_all.at[mine], own_sem.at[0]),
        pltpu.make_async_copy(columns(k_ref, mine, HEAD_DIM), k_all.at[me], own_sem.at[1]),
        pltpu.make_async_copy(columns(v_ref, mine, HEAD_DIM), v_all.at[me], own_sem.at[2]),
    ]
    for copy in own_copies:
        copy.start()
    for own in (True, False):
        for t in range(len(steps)):
            w_copy(t, own).start()

    signal({"vocab": 1 - half})
    for peer in peers[1:]:
        signal({"cp": first + peer})

    @pl.when(plane < end)
    def _():
        signal({"cp": me + kv_heads})

    @pl.when(plane > 0)
    def _():
        signal({"cp": me - kv_heads})

    lines = jnp.minimum(plane, 1) + jnp.minimum(end - plane, 1)
    pl.semaphore_wait(pltpu.get_barrier_semaphore(), kv_heads + lines)
    for copy in loads:
        copy.wait()

    def g_copy(r):
        rows = pl.ds(*cuts[r])
        return pltpu.make_async_remote_copy(
            src_ref=own_g.at[rows], dst_ref=other_g.at[rows],
            send_sem=g_sem.at[0, r], recv_sem=g_sem.at[1, r],
            device_id={"vocab": 1 - half}, device_id_type=MESH,
        )

    def plane_copy(idx, i):
        return pltpu.make_async_remote_copy(
            src_ref=columns((own_k, own_v)[i], peers[idx], HEAD_DIM),
            dst_ref=(k_all, v_all)[i].at[me],
            send_sem=plane_sem.at[i, idx], recv_sem=kv_sem.at[i, me],
            device_id={"cp": first + peers[idx]}, device_id_type=MESH,
        )

    def line_copy(left, hops, idx, i):
        block = me - mine + peers[idx] + (kv_heads if left else -kv_heads) * hops
        kept = (k_all, v_all)[i]
        own = hops == 0 and idx == 0
        return pltpu.make_async_remote_copy(
            src_ref=columns((own_k, own_v)[i], mine, HEAD_DIM) if own else kept.at[block],
            dst_ref=kept.at[block],
            send_sem=line_sem.at[left, i, hops * kv_heads + idx], recv_sem=kv_sem.at[i, block],
            device_id={"cp": me + (-kv_heads if left else kv_heads)}, device_id_type=MESH,
        )

    def arrived(block):
        for i in range(2):
            slot = (k_all, v_all)[i].at[block]
            pltpu.make_async_remote_copy(
                src_ref=slot, dst_ref=slot,
                send_sem=plane_sem.at[i, 0], recv_sem=kv_sem.at[i, block],
                device_id={"cp": first + peers[1]}, device_id_type=MESH,
            ).wait_recv()

    def start_line(left, hops, idx):
        for i in range(2):
            line_copy(left, hops, idx, i).start()

    def open_line(idx):
        @pl.when(plane < end)
        def _():
            start_line(0, 0, idx)

        @pl.when(plane > 0)
        def _():
            start_line(1, 0, idx)

    def pass_plane(idx):
        arrived(first + peers[idx])
        open_line(idx)

    def pass_line(hops, idx):
        @pl.when((plane >= hops) & (plane < end))
        def _():
            arrived(first + peers[idx] - hops * kv_heads)
            start_line(0, hops, idx)

        @pl.when((plane <= end - hops) & (plane > 0))
        def _():
            arrived(first + peers[idx] + hops * kv_heads)
            start_line(1, hops, idx)

    def q_copy(idx):
        return pltpu.make_async_remote_copy(
            src_ref=columns(own_q, peers[idx], wide), dst_ref=q_all.at[mine],
            send_sem=q_sems.at[0, idx], recv_sem=q_sems.at[1, idx],
            device_id={"cp": first + peers[idx]}, device_id_type=MESH,
        )

    def u_copy(r, idx):
        rows = pl.ds(*cuts[r])
        return pltpu.make_async_remote_copy(
            src_ref=u_buf.at[idx, rows], dst_ref=u_all.at[mine, rows],
            send_sem=u_sems.at[0, r, idx], recv_sem=u_sems.at[1, r, idx],
            device_id={"cp": first + peers[idx]}, device_id_type=MESH,
        )

    for r in range(len(cuts)):
        g_copy(r).start()
    open_line(0)
    for idx in order[:-1]:
        for i in range(2):
            plane_copy(idx, i).start()
    for idx in order[:-1]:
        q_copy(idx).start()

    half_way = len(steps) // 2
    for t in range(len(steps)):
        w_copy(t, True).wait()
        partial[t] = dot(own_g[...], own_w[t], NT)
        if t == half_way - 1:
            pass_plane(1)
    pass_plane(2)
    pass_plane(3)
    events = [(hops, idx) for hops in range(1, end) for idx in range(kv_heads)]
    slots = len(cuts) * len(steps) // 2
    done = 0
    for r, (start, size) in enumerate(cuts):
        rows = pl.ds(start, size)
        g_copy(r).wait_recv()
        for t, (idx, part) in enumerate(steps):
            if r == 0:
                w_copy(t, False).wait()
            block = partial[t, rows] + dot(other_g[rows], other_w[t], NT)
            u_buf[idx, rows, pl.ds(part * cut, cut)] = block.astype(jnp.bfloat16)
            if part == 1:
                if idx != 0:
                    u_copy(r, idx).start()
                at = r * len(steps) // 2 + t // 2 + 1
                while done < len(events) and done * slots < at * len(events):
                    pass_line(*events[done])
                    done += 1
    for hops, idx in events[done:]:
        pass_line(hops, idx)
    u_all[mine] = u_buf[0]

    for hops in range(1, planes):
        for idx in range(kv_heads):
            @pl.when(plane == end)
            def _():
                arrived(first + peers[idx] - hops * kv_heads)

            @pl.when(plane == 0)
            def _():
                arrived(first + peers[idx] + hops * kv_heads)

    for idx in order[:-1]:
        q_copy(idx).wait_recv()
        for r in range(len(cuts)):
            u_copy(r, idx).wait()
    for copy in own_copies:
        copy.wait()
    for r in range(len(cuts)):
        g_copy(r).wait_send()
    for idx in order[:-1]:
        q_copy(idx).wait_send()
        for i in range(2):
            plane_copy(idx, i).wait_send()
    for hops in range(end):
        for idx in range(kv_heads):
            for i in range(2):
                @pl.when((plane >= hops) & (plane < end))
                def _():
                    line_copy(0, hops, idx, i).wait_send()

                @pl.when((plane <= end - hops) & (plane > 0))
                def _():
                    line_copy(1, hops, idx, i).wait_send()


def score_kernel(
    order_ref, q_ref, k_ref, v_ref, u_ref, w_out, g_out, q_stack, u_stack,
    places, ks, vs, s_buf, p_buf,
):
    plane = lax.axis_index("cp") // q_ref.shape[0]
    own_rows = q_ref.shape[1]
    groups = q_ref.shape[2] // HEAD_DIM
    seq = k_ref.shape[0]
    spans = order_ref.shape[0]
    rows = seq // spans
    tile = groups * rows
    own_spans = q_ref.shape[0] * own_rows // rows
    per_block = own_rows // rows
    per_tile = TILE // rows
    scale = HEAD_DIM ** (-0.5) * 1.4426950408889634

    for r in range(spans):
        places[order_ref[r]] = r

    def place(j):
        return pl.ds(pl.multiple_of(places[j] * rows, rows), rows)

    for j in range(spans):
        for target, ref in ((ks, k_ref), (vs, v_ref)):
            target[pl.ds(j * rows, rows), :] = ref[place(j), :]

    def fold(x, op):
        return op(x.reshape(TILE // 8, 8, tile), axis=0)

    key_at = lax.broadcasted_iota(jnp.int32, (TILE, tile), 0)
    query_at = lax.rem(lax.broadcasted_iota(jnp.int32, (TILE, tile), 1), rows)

    def one_span(t, carry):
        block = t // per_block
        own = pl.ds(pl.multiple_of(lax.rem(t, per_block) * rows, rows), rows)
        cols = pl.ds(pl.multiple_of(t * tile, tile), tile)
        start = order_ref[plane * own_spans + t] * rows

        def stacked(ref):
            return jnp.concatenate(
                [ref[block, own, h * HEAD_DIM : (h + 1) * HEAD_DIM] for h in range(groups)], axis=0
            )

        def with_keys(last):
            q_tile = stacked(q_ref)
            u_tile = stacked(u_ref)
            q_stack[cols, :] = q_tile
            u_stack[cols, :] = u_tile
            peak = None
            for j in range(last + 1):
                keys = pl.ds(j * TILE, TILE)
                s = dot(ks[keys, :], q_tile, NT)
                if j == last:
                    s = jnp.where(key_at + (last * TILE - start) <= query_at, s, -1e30)
                s_buf[keys, :] = s
                top = fold(s, jnp.max)
                peak = top if peak is None else jnp.maximum(peak, top)
            peak = jnp.max(peak, axis=0, keepdims=True)
            total = jnp.zeros((8, tile), jnp.float32)
            delta = jnp.zeros((8, tile), jnp.float32)
            for j in range(last + 1):
                keys = pl.ds(j * TILE, TILE)
                p = jnp.exp2((s_buf[keys, :] - peak) * scale)
                dp = dot(vs[keys, :], u_tile, NT)
                total = total + fold(p, jnp.sum)
                delta = delta + fold(p * dp, jnp.sum)
                s_buf[keys, :] = p
                p_buf[keys, :] = dp
            inverse = 1.0 / jnp.sum(total, axis=0, keepdims=True)
            delta = jnp.sum(delta, axis=0, keepdims=True) * inverse
            for j in range(last + 1):
                keys = pl.ds(j * TILE, TILE)
                w = s_buf[keys, :] * inverse
                g = (w * (p_buf[keys, :] - delta)).astype(jnp.bfloat16)
                w = w.astype(jnp.bfloat16)
                for i in range(per_tile):
                    at = place(j * per_tile + i)
                    w_out[at, cols] = w[i * rows : (i + 1) * rows]
                    g_out[at, cols] = g[i * rows : (i + 1) * rows]
            blank = jnp.zeros((rows, tile), jnp.bfloat16)
            for j in range((last + 1) * per_tile, spans):
                w_out[place(j), cols] = blank
                g_out[place(j), cols] = blank

        for last in range(seq // TILE):
            pl.when(start // TILE == last)(functools.partial(with_keys, last))
        return carry

    lax.fori_loop(0, own_spans, one_span, 0)


def return_kernel(
    planes, kv_heads, w_ref, g_ref, q_ref, u_ref, k_ref, dq_all, dk_out, dv_out,
    k_turned, terms, summed, inbox, plane_box, dq_buf,
    send_sem, recv_sem, plane_sems, q_sems,
):
    me = lax.axis_index("cp")
    mine = lax.rem(me, kv_heads)
    plane = me // kv_heads
    first = plane * kv_heads
    end = planes - 1
    high = plane // 2
    outer = (plane == 0) | (plane == end)
    inner = 2 - high
    near = 1 + high
    peers = neighbours(mine)
    block_rows, wide = dq_buf.shape[1:]
    groups = wide // HEAD_DIM
    seq = g_ref.shape[0]
    tile = 2 * HEAD_DIM
    rows = tile // groups
    factor = HEAD_DIM ** (-0.5)

    for peer in peers[1:]:
        signal({"cp": first + peer})

    @pl.when(plane < end)
    def _():
        for m in range(kv_heads):
            signal({"cp": first + kv_heads + m})

    @pl.when(plane > 0)
    def _():
        for m in range(kv_heads):
            signal({"cp": first - kv_heads + m})

    def remote(source, target, sent, got, device):
        return pltpu.make_async_remote_copy(
            src_ref=source, dst_ref=target, send_sem=sent, recv_sem=got,
            device_id={"cp": device}, device_id_type=MESH,
        )

    def relay(source, stage, j, way, hops, device):
        slot = hops * kv_heads + j
        return remote(
            source, inbox.at[way, slot], send_sem.at[stage, j], recv_sem.at[way, slot],
            device * kv_heads + mine,
        )

    def final(source, stage, j, way, device):
        return remote(
            source, inbox.at[way, mine], send_sem.at[stage, j], recv_sem.at[way, mine],
            device * kv_heads + j,
        )

    def arrived(way, slot):
        at = inbox.at[way, slot]
        remote(at, at, send_sem.at[0, 0], recv_sem.at[way, slot], first + peers[1]).wait_recv()

    def chunk_of(i):
        return (1 - high) * (end - i) + high * i

    def compute(i):
        def one(j, carry):
            block = chunk_of(i) * kv_heads + j
            keys = pl.ds(pl.multiple_of(block * block_rows, block_rows), block_rows)
            dk = dot(g_ref[keys, :], q_ref[...], NN) * factor
            dv = dot(w_ref[keys, :], u_ref[...], NN)
            terms[block, :, :HEAD_DIM] = dk.astype(jnp.bfloat16)
            terms[block, :, HEAD_DIM:] = dv.astype(jnp.bfloat16)
            return carry

        lax.fori_loop(0, kv_heads, one, 0)

    def outward(i, j):
        source = terms.at[chunk_of(i) * kv_heads + j]
        if i == end - 1:
            return final(source, i, j, high, near)
        return relay(source, i, j, high, end - 1 - i, near)

    def plane_copy(idx):
        return remote(
            terms.at[first + peers[idx]], plane_box.at[mine],
            plane_sems.at[0, idx], plane_sems.at[1, mine], first + peers[idx],
        )

    def plane_arrived(idx):
        at = plane_box.at[peers[idx]]
        remote(at, at, plane_sems.at[0, idx], plane_sems.at[1, peers[idx]], first + peers[idx]).wait_recv()

    def dq_copy(idx):
        return remote(
            dq_buf.at[peers[idx]], columns(dq_all, mine, wide),
            q_sems.at[0, idx], q_sems.at[1, idx], first + peers[idx],
        )

    for i in range(planes):
        compute(i)
        if i == 0:
            lines = jnp.minimum(plane, 1) + jnp.minimum(end - plane, 1)
            pl.semaphore_wait(
                pltpu.get_barrier_semaphore(), kv_heads - 1 + kv_heads * lines
            )
        if i < end:
            @pl.when(outer)
            def _():
                for j in range(kv_heads):
                    outward(i, j).start()
    for idx in (2, 3, 1):
        plane_copy(idx).start()

    def middle(stage, way, slot, chunk, copy):
        for j in range(kv_heads):
            arrived(way, slot * kv_heads + j)
            total = terms[chunk * kv_heads + j].astype(jnp.float32) + inbox[
                way, slot * kv_heads + j
            ].astype(jnp.float32)
            summed[stage, j] = total.astype(jnp.bfloat16)
            copy(j).start()

    def onward(j):
        return relay(summed.at[0, j], 0, j, high, 1, inner)

    def to_end(j):
        return final(summed.at[1, j], 1, j, 1 - high, high * end)

    def to_inner(j):
        return final(summed.at[2, j], 2, j, high, inner)

    k_turned[...] = k_ref[...].T
    for t in range(seq // tile):
        cols = slice(t * tile, (t + 1) * tile)
        part = dot(k_turned[...], g_ref[:, cols], NN)
        part = (part.T * factor).astype(jnp.bfloat16)
        block, at = divmod(t * rows, block_rows)
        for h in range(groups):
            dq_buf[block, at : at + rows, h * HEAD_DIM : (h + 1) * HEAD_DIM] = part[
                h * rows : (h + 1) * rows
            ]
    for idx in (2, 3, 1):
        dq_copy(idx).start()

    @pl.when(jnp.logical_not(outer))
    def _():
        middle(0, high, 2, (1 - high) * end, onward)
        middle(1, 1 - high, 1, high * end, to_end)
        middle(2, high, 1, inner, to_inner)

    dq_all[:, pl.ds(pl.multiple_of(mine * wide, wide), wide)] = dq_buf[mine]
    plane_box[mine] = terms[me]

    def add(ref, m, value, fresh):
        cols = slice(m * HEAD_DIM, (m + 1) * HEAD_DIM)
        ref[:, cols] = value if fresh else ref[:, cols] + value

    def collect(box, m, fresh):
        value = box.astype(jnp.float32)
        add(dk_out, m, value[:, :HEAD_DIM], fresh)
        add(dv_out, m, value[:, HEAD_DIM:], fresh)

    for idx in range(1, kv_heads):
        plane_arrived(idx)
    for m in range(kv_heads):
        collect(plane_box[m], m, True)

    @pl.when(plane < end)
    def _():
        for m in range(kv_heads):
            arrived(1, m)
            collect(inbox[1, m], m, False)

    @pl.when(plane > 0)
    def _():
        for m in range(kv_heads):
            arrived(0, m)
            collect(inbox[0, m], m, False)

    for idx in range(1, kv_heads):
        plane_copy(idx).wait_send()
        dq_copy(idx).wait()

    @pl.when(outer)
    def _():
        for i in range(end):
            for j in range(kv_heads):
                outward(i, j).wait_send()

    @pl.when(jnp.logical_not(outer))
    def _():
        for copy in (onward, to_end, to_inner):
            for j in range(kv_heads):
                copy(j).wait_send()


def by_planes(n, queries, key_states, value_states, out_grad, o_weight, span_order):
    own_rows, width = queries.shape
    kv_heads = key_states.shape[1] // HEAD_DIM
    planes = n // kv_heads
    wide = width // kv_heads
    cut = wide // 2
    seq = own_rows * n
    tile = (HEADS // KV_HEADS) * (seq // span_order.shape[0])
    stack = kv_heads * own_rows * (HEADS // KV_HEADS)
    quarter = own_rows // 4
    cuts = ((0, 2 * quarter), (2 * quarter, quarter), (3 * quarter, quarter))
    any_spec = pl.BlockSpec(memory_space=pl.ANY)
    vmem_spec = pl.BlockSpec(memory_space=pltpu.VMEM)
    smem_spec = pl.BlockSpec(memory_space=pltpu.SMEM)
    dma = pltpu.SemaphoreType.DMA
    low = jnp.bfloat16
    q_block = pltpu.VMEM((kv_heads, own_rows, wide), low)
    kv_block = pltpu.VMEM((n, own_rows, HEAD_DIM), low)
    q_all, k_all, v_all, u_all = pl.pallas_call(
        functools.partial(send_kernel, planes, kv_heads, cuts),
        out_shape=(q_block, kv_block, kv_block, q_block),
        in_specs=[any_spec] * 5,
        out_specs=(vmem_spec,) * 4,
        scratch_shapes=[
            pltpu.VMEM((own_rows, width), low),
            pltpu.VMEM(key_states.shape, low),
            pltpu.VMEM(key_states.shape, low),
            pltpu.VMEM((own_rows, width), low),
            pltpu.VMEM((own_rows, width), low),
            pltpu.VMEM((2 * kv_heads, cut, width), low),
            pltpu.VMEM((2 * kv_heads, cut, width), low),
            pltpu.VMEM((2 * kv_heads, own_rows, cut), jnp.float32),
            pltpu.VMEM((kv_heads, own_rows, wide), low),
            dma((4,)),
            dma((3,)),
            dma((2, 2 * kv_heads)),
            dma((2, len(cuts))),
            dma((2, kv_heads)),
            dma((2, 2, (planes - 1) * kv_heads)),
            dma((2, n)),
            dma((2, kv_heads)),
            dma((2, len(cuts), kv_heads)),
        ],
        compiler_params=pltpu.CompilerParams(
            collective_id=0, has_side_effects=True, vmem_limit_bytes=SEND_LIMIT
        ),
        name="send_heads",
    )(queries, key_states, value_states, out_grad, o_weight)
    k_all = k_all.reshape(seq, HEAD_DIM)
    pair = jax.ShapeDtypeStruct((seq, stack), low)
    side = jax.ShapeDtypeStruct((stack, HEAD_DIM), low)
    weights, grads, q_stack, u_stack = pl.pallas_call(
        score_kernel,
        out_shape=(pair, pair, side, side),
        in_specs=[smem_spec] + [vmem_spec] * 4,
        out_specs=(vmem_spec,) * 4,
        scratch_shapes=[pltpu.SMEM(span_order.shape, jnp.int32)]
        + [pltpu.VMEM((seq, HEAD_DIM), low)] * 2
        + [pltpu.VMEM((seq, tile), jnp.float32)] * 2,
        compiler_params=pltpu.CompilerParams(vmem_limit_bytes=16 << 20),
        name="scores",
    )(span_order, q_all, k_all, v_all.reshape(seq, HEAD_DIM), u_all)
    term = (own_rows, 2 * HEAD_DIM)
    grad = jax.ShapeDtypeStruct(key_states.shape, jnp.float32)
    dq_all, key_grad, value_grad = pl.pallas_call(
        functools.partial(return_kernel, planes, kv_heads),
        out_shape=(jax.ShapeDtypeStruct((own_rows, width), low), grad, grad),
        in_specs=[vmem_spec] * 5,
        out_specs=(vmem_spec,) * 3,
        scratch_shapes=[
            pltpu.VMEM((HEAD_DIM, seq), low),
            pltpu.VMEM((n,) + term, low),
            pltpu.VMEM((3, kv_heads) + term, low),
            pltpu.VMEM((2, 3 * kv_heads) + term, low),
            pltpu.VMEM((kv_heads,) + term, low),
            pltpu.VMEM((kv_heads, own_rows, wide), low),
            dma((3, kv_heads)),
            dma((2, 3 * kv_heads)),
            dma((2, kv_heads)),
            dma((2, kv_heads)),
        ],
        compiler_params=pltpu.CompilerParams(
            collective_id=1, has_side_effects=True, vmem_limit_bytes=16 << 20
        ),
        name="return_grads",
    )(weights, grads, q_stack, u_stack, k_all)
    return (dq_all.astype(jnp.float32), key_grad, value_grad)


SEND_LIMIT = 60 << 20


def solution(mesh):
    n = mesh.shape["cp"]
    planes = mesh.shape["vocab"] == 2 and n == 4 * (KV_HEADS // 2)
    body = functools.partial(by_planes, n) if planes else local
    return jax.shard_map(
        body,
        mesh=mesh,
        in_specs=(
            P("cp", "vocab"),
            P("cp", "vocab"),
            P("cp", "vocab"),
            P("cp", "vocab"),
            P("vocab", None),
            P(),
        ),
        out_specs=(P("cp", "vocab"), P("cp", "vocab"), P("cp", "vocab")),
        check_vma=False,
    )
```

time: 72.6 us -> 68.6 us (0.945); the launches traced: 71.1 us -> 68.3 us
  local copies, waits for them, and re-layouts: 3.89 us -> 1.41 us
  other arithmetic: 2 us -> 1.08 us
    unnamed x10 -> x4, local copies, waits for them, and re-layouts: 3.89 us -> 1.41 us
    concatenate x1 -> x0, other arithmetic: 0.83 us -> none  [over_planes(): return jnp.concatenate(heads, axis=1)]
where the time goes in v1:
time: 68.6 us; the launch traced here: 68.3 us
  Pallas kernels  65.2 us (95%)
  local copies, waits for them, and re-layouts  1.41 us (2%)
  other arithmetic  1.08 us (2%)
    pallas_call x1, Pallas kernels, by_planes(): pl.pallas_call(functools.partial(send_kernel, planes, kv_heads, cuts), ou...  28.3 us
    pallas_call x1, Pallas kernels, by_planes(): pl.pallas_call(functools.partial(return_kernel, planes, kv_heads), out_sh...  27.2 us
    pallas_call x1, Pallas kernels, by_planes(): pl.pallas_call(score_kernel, out_shape=(pair, pair, side, side), in_specs...  9.67 us
    unnamed x4, local copies, waits for them, and re-layouts  1.41 us

profile of v1, /device:TPU:13, one launch (start us, length us, event | category | flops | bytes accessed | tf_op | source)
XLA Modules:
  0.0 68.3 jit_solution(13694730312662674381)
XLA Ops:
  0.6 0.0 copy-start
  0.6 28.3 %send_heads.1 = (bf16[4,128,512]{2,1,0:T(8,128)(2,1)S(1)}, bf16[16,128,128]{2,1,0:T(8,128)(2,1)S(1)}, bf16[16,128,128]{2,1,0:T(8,128)(2,1)S(1)}, bf16[4,128,512]{2,1,0:T(8,128)(2,1)S(1)}) custom-call(bf16[128,2048]{1,0:T(8,128)(2,1)} %q_ref.1, bf16[128,512]{1,0:T(8,128)(2,1)} %k_ref.1, bf16[128,512]{1,0:T(8,128)(2,1)} %v_ref.1, bf16[128,2048]{1,0:T(8,128)(2,1)} %g_ref.1, ...), custom_call_target="tpu_custom_call" | custom-call | tf_op jit(solution)/shard_map/send_heads/pallas_call | solution.py:683
  28.9 0.0 copy-done
  28.9 9.7 %scores.1 = (bf16[2048,2048]{1,0:T(8,128)(2,1)S(1)}, bf16[2048,2048]{1,0:T(8,128)(2,1)S(1)}, bf16[2048,128]{1,0:T(8,128)(2,1)S(1)}, bf16[2048,128]{1,0:T(8,128)(2,1)S(1)}) custom-call(s32[32]{0:T(128)S(1)} %copy-done, bf16[4,128,512]{2,1,0:T(8,128)(2,1)S(1)} %get-tuple-element.14.q_ref, bf16[2048,128]{1,0:T(8,128)(2,1)S(1)} %bitcast.2, ...), custom_call_target="tpu_custom_call" | custom-call | tf_op jit(solution)/shard_map/scores/pallas_call | solution.py:716
  38.6 27.2 %return_grads.1 = (bf16[128,2048]{1,0:T(8,128)(2,1)S(1)}, f32[128,512]{1,0:T(8,128)S(1)}, f32[128,512]{1,0:T(8,128)S(1)}) custom-call(bf16[2048,2048]{1,0:T(8,128)(2,1)S(1)} %get-tuple-element.18.w_ref, bf16[2048,2048]{1,0:T(8,128)(2,1)S(1)} %get-tuple-element.19.g_ref, bf16[2048,128]{1,0:T(8,128)(2,1)S(1)} %get-tuple-element.20.q_ref, ...), custom_call_target="tpu_custom_call" | custom-call | tf_op jit(solution)/shard_map/return_grads/pallas_call | solution.py:729
  65.8 1.1 %convert_element_type.3 = f32[128,2048]{1,0:T(8,128)} convert(bf16[128,2048]{1,0:T(8,128)(2,1)S(1)} %get-tuple-element.22) | non-fusion elementwise | flops 262144 | bytes 1572864 | tf_op jit(solution)/shard_map/convert_element_type | solution.py:751
  66.9 0.7 %copy.11 = f32[128,512]{1,0:T(8,128)} copy(f32[128,512]{1,0:T(8,128)S(1)} %get-tuple-element.29) | data formatting | bytes 524288
  67.6 0.7 %copy.12 = f32[128,512]{1,0:T(8,128)} copy(f32[128,512]{1,0:T(8,128)S(1)} %get-tuple-element.30) | data formatting | bytes 524288
Async XLA Ops:
  0.6 28.3 %copy-start = (s32[32]{0:T(128)S(1)}, s32[32]{0:T(128)}, u32[]{:S(2)}) copy-start(s32[32]{0:T(128)} %order_ref.1) | copy-start | bytes 388

commit v2 on v1

--- a/solution.py
+++ b/solution.py
@@ -205,26 +205,25 @@
     ]
     for copy in own_copies:
         copy.start()
+    signal({"vocab": 1 - half})
+    for peer in peers[1:]:
+        signal({"cp": first + peer})
+
+    @pl.when(plane < end)
+    def _():
+        signal({"cp": me + kv_heads})
+
+    @pl.when(plane > 0)
+    def _():
+        signal({"cp": me - kv_heads})
+
+    lines = jnp.minimum(plane, 1) + jnp.minimum(end - plane, 1)
+    for copy in loads:
+        copy.wait()
     for own in (True, False):
         for t in range(len(steps)):
             w_copy(t, own).start()
-
-    signal({"vocab": 1 - half})
-    for peer in peers[1:]:
-        signal({"cp": first + peer})
-
-    @pl.when(plane < end)
-    def _():
-        signal({"cp": me + kv_heads})
-
-    @pl.when(plane > 0)
-    def _():
-        signal({"cp": me - kv_heads})
-
-    lines = jnp.minimum(plane, 1) + jnp.minimum(end - plane, 1)
     pl.semaphore_wait(pltpu.get_barrier_semaphore(), kv_heads + lines)
-    for copy in loads:
-        copy.wait()
 
     def g_copy(r):
         rows = pl.ds(*cuts[r])

time: 68.6 us -> 63.6 us (0.927)
  Pallas kernels: 65.2 us -> 60.2 us
    pallas_call x1, Pallas kernels: 28.3 us -> 24.1 us  [by_planes(): pl.pallas_call(functools.partial(send_kernel, planes, kv_heads, cuts), ou...]
where the time goes in v2:
time: 63.6 us; the launch traced here: 63.3 us
  Pallas kernels  60.2 us (95%)
  local copies, waits for them, and re-layouts  1.41 us (2%)
  other arithmetic  1.08 us (2%)
  between operations  0.67 us (1%)
    pallas_call x1, Pallas kernels, by_planes(): pl.pallas_call(functools.partial(return_kernel, planes, kv_heads), out_sh...  26.6 us
    pallas_call x1, Pallas kernels, by_planes(): pl.pallas_call(functools.partial(send_kernel, planes, kv_heads, cuts), ou...  24.1 us
    pallas_call x1, Pallas kernels, by_planes(): pl.pallas_call(score_kernel, out_shape=(pair, pair, side, side), in_specs...  9.53 us
    unnamed x4, local copies, waits for them, and re-layouts  1.41 us

profile of v2, /device:TPU:13, one launch (start us, length us, event | category | flops | bytes accessed | tf_op | source)
XLA Modules:
  0.0 63.3 jit_solution(10797124424391111722)
XLA Ops:
  0.6 0.0 copy-start
  0.6 24.1 %send_heads.1 = (bf16[4,128,512]{2,1,0:T(8,128)(2,1)S(1)}, bf16[16,128,128]{2,1,0:T(8,128)(2,1)S(1)}, bf16[16,128,128]{2,1,0:T(8,128)(2,1)S(1)}, bf16[4,128,512]{2,1,0:T(8,128)(2,1)S(1)}) custom-call(bf16[128,2048]{1,0:T(8,128)(2,1)} %q_ref.1, bf16[128,512]{1,0:T(8,128)(2,1)} %k_ref.1, bf16[128,512]{1,0:T(8,128)(2,1)} %v_ref.1, bf16[128,2048]{1,0:T(8,128)(2,1)} %g_ref.1, ...), custom_call_target="tpu_custom_call" | custom-call | tf_op jit(solution)/shard_map/send_heads/pallas_call | solution.py:682
  24.7 0.0 copy-done
  24.7 9.5 %scores.1 = (bf16[2048,2048]{1,0:T(8,128)(2,1)S(1)}, bf16[2048,2048]{1,0:T(8,128)(2,1)S(1)}, bf16[2048,128]{1,0:T(8,128)(2,1)S(1)}, bf16[2048,128]{1,0:T(8,128)(2,1)S(1)}) custom-call(s32[32]{0:T(128)S(1)} %copy-done, bf16[4,128,512]{2,1,0:T(8,128)(2,1)S(1)} %get-tuple-element.14.q_ref, bf16[2048,128]{1,0:T(8,128)(2,1)S(1)} %bitcast.2, ...), custom_call_target="tpu_custom_call" | custom-call | tf_op jit(solution)/shard_map/scores/pallas_call | solution.py:715
  34.3 26.6 %return_grads.1 = (bf16[128,2048]{1,0:T(8,128)(2,1)S(1)}, f32[128,512]{1,0:T(8,128)S(1)}, f32[128,512]{1,0:T(8,128)S(1)}) custom-call(bf16[2048,2048]{1,0:T(8,128)(2,1)S(1)} %get-tuple-element.18.w_ref, bf16[2048,2048]{1,0:T(8,128)(2,1)S(1)} %get-tuple-element.19.g_ref, bf16[2048,128]{1,0:T(8,128)(2,1)S(1)} %get-tuple-element.20.q_ref, ...), custom_call_target="tpu_custom_call" | custom-call | tf_op jit(solution)/shard_map/return_grads/pallas_call | solution.py:728
  60.8 1.1 %convert_element_type.3 = f32[128,2048]{1,0:T(8,128)} convert(bf16[128,2048]{1,0:T(8,128)(2,1)S(1)} %get-tuple-element.22) | non-fusion elementwise | flops 262144 | bytes 1572864 | tf_op jit(solution)/shard_map/convert_element_type | solution.py:750
  61.9 0.7 %copy.11 = f32[128,512]{1,0:T(8,128)} copy(f32[128,512]{1,0:T(8,128)S(1)} %get-tuple-element.29) | data formatting | bytes 524288
  62.6 0.7 %copy.12 = f32[128,512]{1,0:T(8,128)} copy(f32[128,512]{1,0:T(8,128)S(1)} %get-tuple-element.30) | data formatting | bytes 524288
Async XLA Ops:
  0.6 24.1 %copy-start = (s32[32]{0:T(128)S(1)}, s32[32]{0:T(128)}, u32[]{:S(2)}) copy-start(s32[32]{0:T(128)} %order_ref.1) | copy-start | bytes 388

commit v3 on v2

--- a/solution.py
+++ b/solution.py
@@ -322,8 +322,9 @@
     pass_plane(2)
     pass_plane(3)
     events = [(hops, idx) for hops in range(1, end) for idx in range(kv_heads)]
-    slots = len(cuts) * len(steps) // 2
-    done = 0
+    done = kv_heads - 1
+    for hops, idx in events[:done]:
+        pass_line(hops, idx)
     for r, (start, size) in enumerate(cuts):
         rows = pl.ds(start, size)
         g_copy(r).wait_recv()
@@ -335,8 +336,7 @@
             if part == 1:
                 if idx != 0:
                     u_copy(r, idx).start()
-                at = r * len(steps) // 2 + t // 2 + 1
-                while done < len(events) and done * slots < at * len(events):
+                if True and done < len(events):
                     pass_line(*events[done])
                     done += 1
     for hops, idx in events[done:]:
@@ -661,6 +661,25 @@
                 copy(j).wait_send()
 
 
+def finish_kernel(dq_ref, dk_ref, dv_ref, dq_out, dk_out, dv_out, wide, sems):
+    parts = wide.shape[0]
+    rows = wide.shape[1]
+    copies = [
+        pltpu.make_async_copy(dk_ref, dk_out, sems.at[parts]),
+        pltpu.make_async_copy(dv_ref, dv_out, sems.at[parts + 1]),
+    ]
+    for copy in copies:
+        copy.start()
+    for i in range(parts):
+        at = pl.ds(i * rows, rows)
+        wide[i] = dq_ref[at, :].astype(jnp.float32)
+        copy = pltpu.make_async_copy(wide.at[i], dq_out.at[at], sems.at[i])
+        copy.start()
+        copies.append(copy)
+    for copy in copies:
+        copy.wait()
+
+
 def by_planes(n, queries, key_states, value_states, out_grad, o_weight, span_order):
     own_rows, width = queries.shape
     kv_heads = key_states.shape[1] // HEAD_DIM
@@ -671,7 +690,7 @@
     tile = (HEADS // KV_HEADS) * (seq // span_order.shape[0])
     stack = kv_heads * own_rows * (HEADS // KV_HEADS)
     quarter = own_rows // 4
-    cuts = ((0, 2 * quarter), (2 * quarter, quarter), (3 * quarter, quarter))
+    cuts = ((0, 2 * quarter), (2 * quarter, 2 * quarter))
     any_spec = pl.BlockSpec(memory_space=pl.ANY)
     vmem_spec = pl.BlockSpec(memory_space=pltpu.VMEM)
     smem_spec = pl.BlockSpec(memory_space=pltpu.SMEM)
@@ -747,7 +766,19 @@
         ),
         name="return_grads",
     )(weights, grads, q_stack, u_stack, k_all)
-    return (dq_all.astype(jnp.float32), key_grad, value_grad)
+    parts = 8
+    return pl.pallas_call(
+        finish_kernel,
+        out_shape=(jax.ShapeDtypeStruct(queries.shape, jnp.float32), grad, grad),
+        in_specs=[vmem_spec] * 3,
+        out_specs=(any_spec,) * 3,
+        scratch_shapes=[
+            pltpu.VMEM((parts, own_rows // parts, width), jnp.float32),
+            dma((parts + 2,)),
+        ],
+        compiler_params=pltpu.CompilerParams(vmem_limit_bytes=8 << 20),
+        name="finish",
+    )(dq_all, key_grad, value_grad)
 
 
 SEND_LIMIT = 60 << 20

time: 63.6 us -> 60.6 us (0.953); the launches traced: 63.3 us -> 61.1 us
  local copies, waits for them, and re-layouts: 1.41 us -> 0.01 us
  other arithmetic: 1.08 us -> 0 us
    unnamed x4 -> x2, local copies, waits for them, and re-layouts: 1.41 us -> 0.01 us
    pallas_call x0 -> x1, Pallas kernels: none -> 1.22 us  [by_planes(): pl.pallas_call(finish_kernel, out_shape=(jax.ShapeDtypeStruct(queries.sha...]
    pallas_call x1, Pallas kernels: 24.1 us -> 23 us  [by_planes(): pl.pallas_call(functools.partial(send_kernel, planes, kv_heads, cuts), ou...]
    convert_element_type x1 -> x0, other arithmetic: 1.08 us -> none  [by_planes(): return (dq_all.astype(jnp.float32), key_grad, value_grad)]
where the time goes in v3:
time: 60.6 us; the launch traced here: 61.1 us
  Pallas kernels  60.2 us (99%)
  between operations  0.83 us (1%)
    pallas_call x1, Pallas kernels, by_planes(): pl.pallas_call(functools.partial(return_kernel, planes, kv_heads), out_sh...  26.3 us
    pallas_call x1, Pallas kernels, by_planes(): pl.pallas_call(functools.partial(send_kernel, planes, kv_heads, cuts), ou...  23 us
    pallas_call x1, Pallas kernels, by_planes(): pl.pallas_call(score_kernel, out_shape=(pair, pair, side, side), in_specs...  9.75 us
    pallas_call x1, Pallas kernels, by_planes(): pl.pallas_call(finish_kernel, out_shape=(jax.ShapeDtypeStruct(queries.sha...  1.22 us

profile of v3, /device:TPU:13, one launch (start us, length us, event | category | flops | bytes accessed | tf_op | source)
XLA Modules:
  0.0 61.1 jit_solution(14321985029464238338)
XLA Ops:
  0.6 0.0 copy-start
  0.6 23.0 %send_heads.1 = (bf16[4,128,512]{2,1,0:T(8,128)(2,1)S(1)}, bf16[16,128,128]{2,1,0:T(8,128)(2,1)S(1)}, bf16[16,128,128]{2,1,0:T(8,128)(2,1)S(1)}, bf16[4,128,512]{2,1,0:T(8,128)(2,1)S(1)}) custom-call(bf16[128,2048]{1,0:T(8,128)(2,1)} %q_ref.1, bf16[128,512]{1,0:T(8,128)(2,1)} %k_ref.1, bf16[128,512]{1,0:T(8,128)(2,1)} %v_ref.1, bf16[128,2048]{1,0:T(8,128)(2,1)} %g_ref.1, ...), custom_call_target="tpu_custom_call" | custom-call | tf_op jit(solution)/shard_map/send_heads/pallas_call | solution.py:701
  23.6 0.0 copy-done
  23.6 9.8 %scores.1 = (bf16[2048,2048]{1,0:T(8,128)(2,1)S(1)}, bf16[2048,2048]{1,0:T(8,128)(2,1)S(1)}, bf16[2048,128]{1,0:T(8,128)(2,1)S(1)}, bf16[2048,128]{1,0:T(8,128)(2,1)S(1)}) custom-call(s32[32]{0:T(128)S(1)} %copy-done, bf16[4,128,512]{2,1,0:T(8,128)(2,1)S(1)} %get-tuple-element.14.q_ref, bf16[2048,128]{1,0:T(8,128)(2,1)S(1)} %bitcast.2, ...), custom_call_target="tpu_custom_call" | custom-call | tf_op jit(solution)/shard_map/scores/pallas_call | solution.py:734
  33.4 26.3 %return_grads.1 = (bf16[128,2048]{1,0:T(8,128)(2,1)S(1)}, f32[128,512]{1,0:T(8,128)S(1)}, f32[128,512]{1,0:T(8,128)S(1)}) custom-call(bf16[2048,2048]{1,0:T(8,128)(2,1)S(1)} %get-tuple-element.18.w_ref, bf16[2048,2048]{1,0:T(8,128)(2,1)S(1)} %get-tuple-element.19.g_ref, bf16[2048,128]{1,0:T(8,128)(2,1)S(1)} %get-tuple-element.20.q_ref, ...), custom_call_target="tpu_custom_call" | custom-call | tf_op jit(solution)/shard_map/return_grads/pallas_call | solution.py:747
  59.7 1.2 %finish.1 = (f32[128,2048]{1,0:T(8,128)}, f32[128,512]{1,0:T(8,128)}, f32[128,512]{1,0:T(8,128)}) custom-call(bf16[128,2048]{1,0:T(8,128)(2,1)S(1)} %get-tuple-element.22.dq_ref, f32[128,512]{1,0:T(8,128)S(1)} %get-tuple-element.23.dk_ref, f32[128,512]{1,0:T(8,128)S(1)} %get-tuple-element.24.dv_ref), custom_call_target="tpu_custom_call" | custom-call | tf_op jit(solution)/shard_map/finish/pallas_call | solution.py:770
Async XLA Ops:
  0.6 23.0 %copy-start = (s32[32]{0:T(128)S(1)}, s32[32]{0:T(128)}, u32[]{:S(2)}) copy-start(s32[32]{0:T(128)} %order_ref.1) | copy-start | bytes 388

commit v4 on v3

--- a/solution.py
+++ b/solution.py
@@ -161,7 +161,7 @@
 
 
 def send_kernel(
-    planes, kv_heads, cuts, q_ref, k_ref, v_ref, g_ref, w_ref, q_all, k_all, v_all, u_all,
+    planes, kv_heads, cuts, pieces, q_ref, k_ref, v_ref, g_ref, w_ref, q_all, k_all, v_all, u_all,
     own_q, own_k, own_v, own_g, other_g, own_w, other_w, partial, u_buf,
     load_sem, own_sem, w_sem, g_sem, plane_sem, line_sem, kv_sem, q_sems, u_sems,
 ):
@@ -225,11 +225,12 @@
             w_copy(t, own).start()
     pl.semaphore_wait(pltpu.get_barrier_semaphore(), kv_heads + lines)
 
-    def g_copy(r):
-        rows = pl.ds(*cuts[r])
+    def g_copy(n):
+        r, inner, size = pieces[n]
+        at = (pl.ds(*cuts[r]), pl.ds(inner, size))
         return pltpu.make_async_remote_copy(
-            src_ref=own_g.at[rows], dst_ref=other_g.at[rows],
-            send_sem=g_sem.at[0, r], recv_sem=g_sem.at[1, r],
+            src_ref=own_g.at[at], dst_ref=other_g.at[at],
+            send_sem=g_sem.at[0, n], recv_sem=g_sem.at[1, n],
             device_id={"vocab": 1 - half}, device_id_type=MESH,
         )
 
@@ -304,8 +305,8 @@
             device_id={"cp": first + peers[idx]}, device_id_type=MESH,
         )
 
-    for r in range(len(cuts)):
-        g_copy(r).start()
+    for n in range(len(pieces)):
+        g_copy(n).start()
     open_line(0)
     for idx in order[:-1]:
         for i in range(2):
@@ -313,32 +314,32 @@
     for idx in order[:-1]:
         q_copy(idx).start()
 
-    half_way = len(steps) // 2
     for t in range(len(steps)):
         w_copy(t, True).wait()
         partial[t] = dot(own_g[...], own_w[t], NT)
-        if t == half_way - 1:
-            pass_plane(1)
-    pass_plane(2)
-    pass_plane(3)
+        if t in (0, 3, 6):
+            pass_plane((0, 3, 6).index(t) + 1)
     events = [(hops, idx) for hops in range(1, end) for idx in range(kv_heads)]
     done = kv_heads - 1
     for hops, idx in events[:done]:
         pass_line(hops, idx)
-    for r, (start, size) in enumerate(cuts):
-        rows = pl.ds(start, size)
-        g_copy(r).wait_recv()
+    for n, (r, inner, size) in enumerate(pieces):
+        rows = pl.ds(*cuts[r])
+        depth = pl.ds(inner, size)
+        g_copy(n).wait_recv()
         for t, (idx, part) in enumerate(steps):
-            if r == 0:
+            if n == 0:
                 w_copy(t, False).wait()
-            block = partial[t, rows] + dot(other_g[rows], other_w[t], NT)
-            u_buf[idx, rows, pl.ds(part * cut, cut)] = block.astype(jnp.bfloat16)
-            if part == 1:
-                if idx != 0:
+            total = partial[t, rows] + dot(other_g[rows, depth], other_w[t, :, depth], NT)
+            if inner + size < width:
+                partial[t, rows] = total
+            else:
+                u_buf[idx, rows, pl.ds(part * cut, cut)] = total.astype(jnp.bfloat16)
+                if part == 1 and idx != 0:
                     u_copy(r, idx).start()
-                if True and done < len(events):
-                    pass_line(*events[done])
-                    done += 1
+            if (n, t) in ((0, 7), (1, 3), (1, 7), (2, 3), (2, 7)) and done < len(events):
+                pass_line(*events[done])
+                done += 1
     for hops, idx in events[done:]:
         pass_line(hops, idx)
     u_all[mine] = u_buf[0]
@@ -359,8 +360,8 @@
             u_copy(r, idx).wait()
     for copy in own_copies:
         copy.wait()
-    for r in range(len(cuts)):
-        g_copy(r).wait_send()
+    for n in range(len(pieces)):
+        g_copy(n).wait_send()
     for idx in order[:-1]:
         q_copy(idx).wait_send()
         for i in range(2):
@@ -691,6 +692,8 @@
     stack = kv_heads * own_rows * (HEADS // KV_HEADS)
     quarter = own_rows // 4
     cuts = ((0, 2 * quarter), (2 * quarter, 2 * quarter))
+    split = width // 2
+    pieces = tuple((r, inner, split) for r in range(len(cuts)) for inner in (0, split))
     any_spec = pl.BlockSpec(memory_space=pl.ANY)
     vmem_spec = pl.BlockSpec(memory_space=pltpu.VMEM)
     smem_spec = pl.BlockSpec(memory_space=pltpu.SMEM)
@@ -699,7 +702,7 @@
     q_block = pltpu.VMEM((kv_heads, own_rows, wide), low)
     kv_block = pltpu.VMEM((n, own_rows, HEAD_DIM), low)
     q_all, k_all, v_all, u_all = pl.pallas_call(
-        functools.partial(send_kernel, planes, kv_heads, cuts),
+        functools.partial(send_kernel, planes, kv_heads, cuts, pieces),
         out_shape=(q_block, kv_block, kv_block, q_block),
         in_specs=[any_spec] * 5,
         out_specs=(vmem_spec,) * 4,
@@ -716,7 +719,7 @@
             dma((4,)),
             dma((3,)),
             dma((2, 2 * kv_heads)),
-            dma((2, len(cuts))),
+            dma((2, len(pieces))),
             dma((2, kv_heads)),
             dma((2, 2, (planes - 1) * kv_heads)),
             dma((2, n)),

time: 60.6 us -> 59.3 us (0.979); the launches traced: 61.1 us -> 59.1 us
  Pallas kernels: 60.2 us -> 58.3 us
    pallas_call x1, Pallas kernels: 26.3 us -> 24.9 us  [by_planes(): pl.pallas_call(functools.partial(return_kernel, planes, kv_heads), out_sh...]
    pallas_call x1, Pallas kernels: 23 us -> 22.4 us  [by_planes(): pl.pallas_call(functools.partial(send_kernel, planes, kv_heads, cuts, pie...]
where the time goes in v4:
time: 59.3 us; the launch traced here: 59.1 us
  Pallas kernels  58.3 us (98%)
  between operations  0.83 us (1%)
    pallas_call x1, Pallas kernels, by_planes(): pl.pallas_call(functools.partial(return_kernel, planes, kv_heads), out_sh...  24.9 us
    pallas_call x1, Pallas kernels, by_planes(): pl.pallas_call(functools.partial(send_kernel, planes, kv_heads, cuts, pie...  22.4 us
    pallas_call x1, Pallas kernels, by_planes(): pl.pallas_call(score_kernel, out_shape=(pair, pair, side, side), in_specs...  9.82 us
    pallas_call x1, Pallas kernels, by_planes(): pl.pallas_call(finish_kernel, out_shape=(jax.ShapeDtypeStruct(queries.sha...  1.22 us

profile of v4, /device:TPU:13, one launch (start us, length us, event | category | flops | bytes accessed | tf_op | source)
XLA Modules:
  0.0 59.1 jit_solution(5415054460923490716)
XLA Ops:
  0.6 0.0 copy-start
  0.6 22.4 %send_heads.1 = (bf16[4,128,512]{2,1,0:T(8,128)(2,1)S(1)}, bf16[16,128,128]{2,1,0:T(8,128)(2,1)S(1)}, bf16[16,128,128]{2,1,0:T(8,128)(2,1)S(1)}, bf16[4,128,512]{2,1,0:T(8,128)(2,1)S(1)}) custom-call(bf16[128,2048]{1,0:T(8,128)(2,1)} %q_ref.1, bf16[128,512]{1,0:T(8,128)(2,1)} %k_ref.1, bf16[128,512]{1,0:T(8,128)(2,1)} %v_ref.1, bf16[128,2048]{1,0:T(8,128)(2,1)} %g_ref.1, ...), custom_call_target="tpu_custom_call" | custom-call | tf_op jit(solution)/shard_map/send_heads/pallas_call | solution.py:704
  23.0 0.0 copy-done
  23.0 9.8 %scores.1 = (bf16[2048,2048]{1,0:T(8,128)(2,1)S(1)}, bf16[2048,2048]{1,0:T(8,128)(2,1)S(1)}, bf16[2048,128]{1,0:T(8,128)(2,1)S(1)}, bf16[2048,128]{1,0:T(8,128)(2,1)S(1)}) custom-call(s32[32]{0:T(128)S(1)} %copy-done, bf16[4,128,512]{2,1,0:T(8,128)(2,1)S(1)} %get-tuple-element.14.q_ref, bf16[2048,128]{1,0:T(8,128)(2,1)S(1)} %bitcast.2, ...), custom_call_target="tpu_custom_call" | custom-call | tf_op jit(solution)/shard_map/scores/pallas_call | solution.py:737
  32.8 24.9 %return_grads.1 = (bf16[128,2048]{1,0:T(8,128)(2,1)S(1)}, f32[128,512]{1,0:T(8,128)S(1)}, f32[128,512]{1,0:T(8,128)S(1)}) custom-call(bf16[2048,2048]{1,0:T(8,128)(2,1)S(1)} %get-tuple-element.18.w_ref, bf16[2048,2048]{1,0:T(8,128)(2,1)S(1)} %get-tuple-element.19.g_ref, bf16[2048,128]{1,0:T(8,128)(2,1)S(1)} %get-tuple-element.20.q_ref, ...), custom_call_target="tpu_custom_call" | custom-call | tf_op jit(solution)/shard_map/return_grads/pallas_call | solution.py:750
  57.7 1.2 %finish.1 = (f32[128,2048]{1,0:T(8,128)}, f32[128,512]{1,0:T(8,128)}, f32[128,512]{1,0:T(8,128)}) custom-call(bf16[128,2048]{1,0:T(8,128)(2,1)S(1)} %get-tuple-element.22.dq_ref, f32[128,512]{1,0:T(8,128)S(1)} %get-tuple-element.23.dk_ref, f32[128,512]{1,0:T(8,128)S(1)} %get-tuple-element.24.dv_ref), custom_call_target="tpu_custom_call" | custom-call | tf_op jit(solution)/shard_map/finish/pallas_call | solution.py:773
Async XLA Ops:
  0.6 22.4 %copy-start = (s32[32]{0:T(128)S(1)}, s32[32]{0:T(128)}, u32[]{:S(2)}) copy-start(s32[32]{0:T(128)} %order_ref.1) | copy-start | bytes 388
